TPU v7x, 128 devices: a whole 4x4x4 slice. The times are simulated.
128 devices in a mesh: group: 4 (over y), dom: 32 (over x, z, core).
Axes of the slice: x: 4, y: 4, z: 4, core: 2. Of those that a mesh axis runs over, the one named last changes fastest.
Arguments:
- p_start: float32 [4096, 128], P(('group', 'dom')), may hold values from -60 to 60
- r_start: float32 [4096, 128], P(('group', 'dom')), may hold values from -60 to 60
- diag_shift: float32 [4096, 128], P(('group', 'dom')), may hold values from 0.5 to 2
- shifts: float32 [8], replicated, may hold values from 0.5 to 1.5
- block_values: float32 [4096, 6, 128, 128], P(('group', 'dom')), may hold values from -0.21875 to 0.21875
- block_cols: int32 [4096, 6], P(('group', 'dom')), may hold values from 0 to 95, as said below
- live_slots: int32 [4096], P(('group', 'dom')), may hold values from 2 to 6, as said below
- needed: int32 [128, 4, 16], P(('group', 'dom')), may hold values from 0 to 31
Outputs:
- basis: float32 [17, 4096, 128], P(None, ('group', 'dom'))
- gram: float32 [17, 17], replicated
Inputs may be any that keep to these rules, and one draw needn't show every extreme that they name: `block_cols`: slot 0 of block row b is the row itself (b mod 32); a value below 32 names a block row of the same device, a value 32 + k * 16 + h names entry h of the device's list k of needed. Devices with dom index 0 never use list 0 in used slots, devices with the last dom index never list 1. Slots from live_slots on hold values in range but are not used. `live_slots`: the first block row of every device uses all 6 slots. needed[d, k] lists the local block rows that device d reads from its source s_k(d), in the order of its extended field.
All inputs are finite; a program needn't handle non-finite values.
Results may differ from a plain program's by a relative error of at most 0.0001.
Values sent between devices are 32-bit elements; how exact they have to be, the bound alone decides.
A program may use at most 64 MiB of HBM per device.

v0:
```python
import functools

import jax
import jax.numpy as jnp
from jax import lax
from jax.experimental import pallas as pl
from jax.experimental.pallas import tpu as pltpu
from jax.sharding import PartitionSpec as P

MESH = pl.DeviceIdType.MESH
UNROLL = 4
GROWS = 24


def split(x):
    high = x.astype(jnp.bfloat16)
    low = (x - high.astype(jnp.float32)).astype(jnp.bfloat16)
    return high, low


def kernel(
    rows, slots, bs, halo, depth, n_group, n_dom,
    p_hbm, r_hbm, diag_hbm, shifts, values_hbm, cols, live, needed,
    basis_hbm, gram_hbm,
    stage, weights, ext_a, ext_b, fields, out, start, diag, index,
    gram_mine, gram_in_a, gram_in_b, gram_in_c, gram_out,
    value_sem, small_sem, out_sem, send_sem, recv_sem, gram_send, gram_recv,
):
    g = lax.axis_index("group")
    m = lax.axis_index("dom")
    column = 8
    n_x = n_dom // column
    x, w = m // column, m % column

    def dom_peer(i):
        return (g, i)

    small = [
        pltpu.make_async_copy(p_hbm, start.at[0], small_sem.at[0]),
        pltpu.make_async_copy(r_hbm, start.at[1], small_sem.at[1]),
        pltpu.make_async_copy(diag_hbm, diag, small_sem.at[2]),
    ]
    for copy in small:
        copy.start()

    def value_copy(b):
        return pltpu.make_async_copy(values_hbm.at[b], stage.at[b], value_sem.at[b])

    def start_values(b, carry):
        value_copy(b).start()
        return carry

    lax.fori_loop(0, rows, start_values, 0)

    neighbours = (
        (g, (m + n_dom - 1) % n_dom),
        (g, (m + 1) % n_dom),
        ((g + n_group - 1) % n_group, m),
        ((g + 1) % n_group, m),
    )
    peers_a = [dom_peer(x * column + (w + j) % column) for j in range(1, column)]
    peers_b = [dom_peer((x + j) % n_x * column + w) for j in range(1, n_x)]
    peers_c = [((g + j) % n_group, m) for j in range(1, n_group)]
    greeted = list(neighbours[:2]) + peers_a + peers_b + peers_c
    barrier = pltpu.get_barrier_semaphore()
    for peer in greeted:
        pl.semaphore_signal(barrier, inc=1, device_id=peer, device_id_type=MESH)

    for copy in small:
        copy.wait()
    width = 2 * rows
    for ext in (ext_a, ext_b):
        ext[5 * width : 5 * width + 16, :] = jnp.zeros((16, bs), jnp.float32)
    ext_a[pl.ds(0, rows, stride=2), :] = start[0]
    ext_a[pl.ds(1, rows, stride=2), :] = start[1]
    pl.semaphore_wait(barrier, len(greeted))

    def field_copies(ext, parity):
        return [
            pltpu.make_async_remote_copy(
                src_ref=ext.at[0:width],
                dst_ref=ext.at[(1 + (k ^ 1)) * width : (2 + (k ^ 1)) * width],
                send_sem=send_sem.at[4 * parity + k],
                recv_sem=recv_sem.at[4 * parity + (k ^ 1)],
                device_id=neighbours[k],
                device_id_type=MESH,
            )
            for k in range(4)
        ]

    for copy in field_copies(ext_a, 0):
        copy.start()

    fields[...] = jnp.zeros(fields.shape, jnp.float32)
    out[0] = start[0]
    out[depth + 1] = start[1]

    def prepare(b, carry):
        value_copy(b).wait()
        for s in range(slots):
            high, low = split(stage[b, s].T)
            weights[b, s * bs : (s + 1) * bs, 0:bs] = high
            weights[b, s * bs : (s + 1) * bs, bs : 2 * bs] = low
        used = live[b]
        for s in range(slots):
            c = cols[b, s]
            far = jnp.maximum(c - rows, 0)
            k, h = far // halo, far % halo
            spot = jnp.where(c < rows, c, (1 + k) * rows + needed[0, k, h])
            index[b * slots + s] = jnp.where(s < used, 2 * spot, 5 * width)
        fields[b, 0:1, :] = start[0, pl.ds(b, 1), :]
        fields[b, depth + 1 : depth + 2, :] = start[1, pl.ds(b, 1), :]
        return carry

    lax.fori_loop(0, rows, prepare, 0)

    def advance(src, dst, step):
        theta = shifts[step - 1]

        def some(i, carry):
            for u in range(UNROLL):
                b = i * UNROLL + u
                parts = []
                for s in range(slots):
                    picked = src[pl.ds(index[b * slots + s], 8), :]
                    high, low = split(picked)
                    parts.append(jnp.concatenate([high, low], axis=0))
                lhs = jnp.concatenate(parts, axis=1)
                y = jnp.dot(lhs, weights[b], preferred_element_type=jnp.float32)
                y = (y[8:16, bs:] + y[8:16, :bs]) + (y[0:8, bs:] + y[0:8, :bs])
                own = src[pl.ds(2 * b, 2), :]
                new = y[0:2] + (diag[pl.ds(b, 1), :] - theta) * own
                dst[pl.ds(2 * b, 2), :] = new
                fields[b, pl.ds(step, 1), :] = new[0:1]
                r_row = jnp.where(step < depth, depth + 1 + step, GROWS - 1)
                fields[b, pl.ds(r_row, 1), :] = new[1:2]
            return carry

        lax.fori_loop(0, rows // UNROLL, some, 0)

    def finish(copies):
        for copy in copies:
            copy.wait_send()

    def pair(i, carry):
        for copy in field_copies(ext_a, 0):
            copy.wait()
        advance(ext_a, ext_b, 2 * i + 1)
        for copy in field_copies(ext_b, 1):
            copy.start()
        out[2 * i + 1] = ext_b[pl.ds(0, rows, stride=2), :]
        out[depth + 1 + 2 * i + 1] = ext_b[pl.ds(1, rows, stride=2), :]
        for copy in field_copies(ext_b, 1):
            copy.wait()
        advance(ext_b, ext_a, 2 * i + 2)

        @pl.when(i < depth // 2 - 1)
        def _():
            for copy in field_copies(ext_a, 0):
                copy.start()
            out[depth + 1 + 2 * i + 2] = ext_a[pl.ds(1, rows, stride=2), :]

        out[2 * i + 2] = ext_a[pl.ds(0, rows, stride=2), :]
        return carry

    lax.fori_loop(0, depth // 2, pair, 0)

    basis_copy = pltpu.make_async_copy(out, basis_hbm, out_sem.at[0])
    basis_copy.start()

    highs, lows = [], []
    for b in range(rows):
        high, low = split(fields[b])
        highs.append(high)
        lows.append(low)
    both = jnp.concatenate(
        [jnp.concatenate(highs, axis=1), jnp.concatenate(lows, axis=1)], axis=0
    )
    prod = lax.dot_general(
        both, both, (((1,), (1,)), ((), ())), preferred_element_type=jnp.float32
    )
    gram = (prod[GROWS:, GROWS:] + prod[GROWS:, :GROWS]) + (prod[:GROWS, GROWS:] + prod[:GROWS, :GROWS])
    gram_mine[0] = jnp.zeros((GROWS, bs), jnp.float32)
    gram_mine[0, :, 0:GROWS] = gram

    phases = (
        (peers_a, column, w, gram_in_a, 0),
        (peers_b, n_x, x, gram_in_b, column),
        (peers_c, n_group, g, gram_in_c, column + n_x),
    )
    total = None
    for number, (peers, count, mine, landing, first) in enumerate(phases):
        copies = [
            pltpu.make_async_remote_copy(
                src_ref=gram_mine.at[number],
                dst_ref=landing.at[mine],
                send_sem=gram_send.at[first + j],
                recv_sem=gram_recv.at[first + j],
                device_id=peer,
                device_id_type=MESH,
            )
            for j, peer in enumerate(peers)
        ]
        for copy in copies:
            copy.start()
        landing[mine] = gram_mine[number]
        for copy in copies:
            copy.wait()
        total = landing[0]
        for i in range(1, count):
            total = total + landing[i]
        if number < 2:
            gram_mine[number + 1] = total
    cells = rows * bs * n_group * n_dom
    gram_out[...] = total * (1.0 / cells)
    gram_copy = pltpu.make_async_copy(gram_out, gram_hbm, out_sem.at[1])
    gram_copy.start()
    gram_copy.wait()
    basis_copy.wait()


def per_device(n_group, n_dom, p_start, r_start, diag_shift, shifts, block_values, block_cols, live_slots, needed):
    rows, bs = p_start.shape
    slots = block_cols.shape[1]
    halo = needed.shape[2]
    depth = shifts.shape[0]
    ncols = 2 * depth + 1
    f32 = jnp.float32
    hbm = pl.BlockSpec(memory_space=pl.ANY)
    smem = pl.BlockSpec(memory_space=pltpu.SMEM)
    dma = pltpu.SemaphoreType.DMA
    basis, gram = pl.pallas_call(
        functools.partial(kernel, rows, slots, bs, halo, depth, n_group, n_dom),
        out_shape=(
            jax.ShapeDtypeStruct((ncols, rows, bs), f32),
            jax.ShapeDtypeStruct((GROWS, bs), f32),
        ),
        in_specs=[hbm, hbm, hbm, smem, hbm, smem, smem, smem],
        out_specs=(hbm, hbm),
        scratch_shapes=[
            pltpu.VMEM((rows, slots, bs, bs), f32),
            pltpu.VMEM((rows, slots * bs, 2 * bs), jnp.bfloat16),
            pltpu.VMEM((10 * rows + 16, bs), f32),
            pltpu.VMEM((10 * rows + 16, bs), f32),
            pltpu.VMEM((rows, GROWS, bs), f32),
            pltpu.VMEM((ncols, rows, bs), f32),
            pltpu.VMEM((2, rows, bs), f32),
            pltpu.VMEM((rows, bs), f32),
            pltpu.SMEM((rows * slots,), jnp.int32),
            pltpu.VMEM((3, GROWS, bs), f32),
            pltpu.VMEM((8, GROWS, bs), f32),
            pltpu.VMEM((n_dom // 8, GROWS, bs), f32),
            pltpu.VMEM((n_group, GROWS, bs), f32),
            pltpu.VMEM((GROWS, bs), f32),
            dma((rows,)),
            dma((3,)),
            dma((2,)),
            dma((8,)),
            dma((8,)),
            dma((16,)),
            dma((16,)),
        ],
        compiler_params=pltpu.CompilerParams(
            collective_id=0, has_side_effects=True, vmem_limit_bytes=60 * 1024 * 1024
        ),
    )(p_start, r_start, diag_shift, shifts, block_values, block_cols, live_slots, needed)
    return basis, gram[:ncols, :ncols]


def solution(mesh):
    both = ("group", "dom")
    in_specs = (
        P(both, None),
        P(both, None),
        P(both, None),
        P(),
        P(both, None, None, None),
        P(both, None),
        P(both),
        P(both, None, None),
    )
    return jax.shard_map(
        functools.partial(per_device, mesh.shape["group"], mesh.shape["dom"]),
        mesh=mesh,
        in_specs=in_specs,
        out_specs=(P(None, both, None), P()),
        check_vma=False,
    )
```

profile of v0, /device:TPU:1, one launch (start us, length us, event | category | flops | bytes accessed | tf_op | source)
XLA Modules:
  0.0 81.1 jit_solution(1130407478927246012)
XLA Ops:
  0.6 1.4 %copy.10.cols = s32[32,6]{1,0:T(8,128)} copy(s32[32,6]{0,1:T(8,128)} %param.13) | data formatting | bytes 1536 | tf_op args[5]
  2.0 76.1 %shard_map.95 = (f32[17,32,128]{2,1,0:T(8,128)}, f32[24,128]{1,0:T(8,128)}) custom-call(f32[32,128]{1,0:T(8,128)} %p_hbm.1, f32[32,128]{1,0:T(8,128)} %r_hbm.1, f32[32,128]{1,0:T(8,128)} %diag_hbm.1, f32[8]{0:T(128)} %shifts.1, f32[32,6,128,128]{3,2,1,0:T(8,128)} %values_hbm.1, s32[32,6]{1,0:T(8,128)} %copy.10.cols, s32[32]{0:T(128)} %live.1, s32[1,4,16]{2,1,0:T(4,128)} %needed.1), custom_call_target="tpu_custom_call" | custom-call | tf_op jit(solution)/shard_map/pallas_call | solution.py:232
  78.1 1.7 %copy.13 = f32[17,32,128]{2,1,0:T(8,128)} copy(f32[17,32,128]{2,1,0:T(8,128)} %get-tuple-element.8) | data formatting | bytes 557056
  79.8 1.3 %copy.14 = f32[17,17]{1,0:T(8,128)} copy(f32[17,17]{1,0:T(8,128)} %bitcast.1) | data formatting | bytes 2312
where the time goes:
time: 82.3 us; the launch traced here: 81.1 us
  Pallas kernels  76.1 us (92%)
  local copies, waits for them, and re-layouts  4.36 us (5%)
    pallas_call x1, Pallas kernels, per_device(): pl.pallas_call(functools.partial(kernel, rows, slots, bs, halo, depth, n_...  76.1 us
    unnamed x3, local copies, waits for them, and re-layouts  4.36 us

commit v1 on v0

v1 whole, which is shorter than its diff:
```python
import functools

import jax
import jax.numpy as jnp
from jax import lax
from jax.experimental import pallas as pl
from jax.experimental.pallas import tpu as pltpu
from jax.sharding import PartitionSpec as P

MESH = pl.DeviceIdType.MESH
UNROLL = 32
GROWS = 24
COLUMN = 8


def split(x):
    high = x.astype(jnp.bfloat16)
    low = (x - high.astype(jnp.float32)).astype(jnp.bfloat16)
    return high, low


def both_halves(x):
    high, low = split(x)
    return jnp.concatenate([high, low], axis=0)


def four_sum(y, bs):
    return (y[8:16, bs:] + y[8:16, :bs]) + (y[0:8, bs:] + y[0:8, :bs])


def kernel(
    rows, slots, bs, halo, depth, n_group, n_dom,
    p_hbm, r_hbm, diag_hbm, shifts, values_hbm, cols, live, needed,
    basis_hbm, gram_hbm,
    stage, weights, ext_a, ext_b, fields, out, start, diag, index, partial,
    gram_mine, gram_in_a, gram_in_b, gram_out,
    value_sem, small_sem, out_sem, send_sem, recv_sem, gram_send, gram_recv,
):
    g = lax.axis_index("group")
    m = lax.axis_index("dom")
    n_x = n_dom // COLUMN
    x, w = m // COLUMN, m % COLUMN
    width = 2 * rows
    nothing = 5 * width

    small = [
        pltpu.make_async_copy(p_hbm, start.at[0], small_sem.at[0]),
        pltpu.make_async_copy(r_hbm, start.at[1], small_sem.at[1]),
        pltpu.make_async_copy(diag_hbm, diag, small_sem.at[2]),
    ]
    for copy in small:
        copy.start()

    neighbours = (
        (g, (m + n_dom - 1) % n_dom),
        (g, (m + 1) % n_dom),
        ((g + n_group - 1) % n_group, m),
        ((g + 1) % n_group, m),
    )
    peers_a = [(g, x * COLUMN + (w + j) % COLUMN) for j in range(1, COLUMN)]
    peers_b = [
        ((g + j // n_x) % n_group, (x + j) % n_x * COLUMN + w) for j in range(1, n_x * n_group)
    ]
    greeted = list(neighbours[:2]) + peers_a + peers_b
    barrier = pltpu.get_barrier_semaphore()
    for peer in greeted:
        pl.semaphore_signal(barrier, inc=1, device_id=peer, device_id_type=MESH)

    def value_copy(b):
        return pltpu.make_async_copy(values_hbm.at[b], stage.at[b], value_sem.at[b])

    def start_values(b, carry):
        value_copy(b).start()
        return carry

    lax.fori_loop(0, rows, start_values, 0)

    for copy in small:
        copy.wait()
    for ext in (ext_a, ext_b):
        ext[nothing : nothing + 16, :] = jnp.zeros((16, bs), jnp.float32)
    ext_a[pl.ds(0, rows, stride=2), :] = start[0]
    ext_a[pl.ds(1, rows, stride=2), :] = start[1]
    fields[...] = jnp.zeros(fields.shape, jnp.float32)

    def field_copies(ext, parity):
        return [
            pltpu.make_async_remote_copy(
                src_ref=ext.at[0:width],
                dst_ref=ext.at[(1 + (k ^ 1)) * width : (2 + (k ^ 1)) * width],
                send_sem=send_sem.at[4 * parity + k],
                recv_sem=recv_sem.at[4 * parity + (k ^ 1)],
                device_id=neighbours[k],
                device_id_type=MESH,
            )
            for k in range(4)
        ]

    def prepare(b, carry):
        value_copy(b).wait()
        for s in range(slots):
            high, low = split(stage[b, s].T)
            weights[b, 0, s * bs : (s + 1) * bs, :] = high
            weights[b, 1, s * bs : (s + 1) * bs, :] = low
        used = live[b]
        for s in range(1, slots):
            c = cols[s, b]
            far = jnp.maximum(c - rows, 0)
            k, h = far // halo, far % halo
            spot = jnp.where(c < rows, c, (1 + k) * rows + needed[0, k, h])
            index[b * slots + s] = jnp.where(s < used, 2 * spot, nothing)
        return carry

    lax.fori_loop(0, rows // 2, prepare, 0)
    pl.semaphore_wait(barrier, len(greeted))
    for copy in field_copies(ext_a, 0):
        copy.start()
    lax.fori_loop(rows // 2, rows, prepare, 0)

    def matrix(b, first, last):
        span = slice(first * bs, last * bs)
        return jnp.concatenate([weights[b, 0, span, :], weights[b, 1, span, :]], axis=1)

    def keep(src, step):
        out[step] = src[pl.ds(0, rows, stride=2), :]
        r_row = jnp.where(step < depth, depth + 1 + step, GROWS - 1)

        @pl.when(step < depth)
        def _():
            out[depth + 1 + step] = src[pl.ds(1, rows, stride=2), :]

        for b in range(rows):
            fields[b, pl.ds(step, 1), :] = src[2 * b : 2 * b + 1, :]
            fields[b, pl.ds(r_row, 1), :] = src[2 * b + 1 : 2 * b + 2, :]

    def ahead(src, step):
        theta = shifts[step]
        for first in range(0, rows, 4):
            own = src[2 * first : 2 * first + 8, :]
            lhs = both_halves(own)
            for j in range(4):
                b, two = first + j, slice(2 * j, 2 * j + 2)
                y = jnp.dot(lhs, matrix(b, 0, 1), preferred_element_type=jnp.float32)
                near = four_sum(y, bs)[two] + (diag[b : b + 1, :] - theta) * own[two]
                partial[2 * b : 2 * b + 2, :] = near

    def advance(src, dst):
        def some(i, carry):
            for u in range(UNROLL):
                b = i * UNROLL + u
                lhs = jnp.concatenate(
                    [
                        both_halves(src[pl.ds(index[b * slots + s], 8), :])
                        for s in range(1, slots)
                    ],
                    axis=1,
                )
                y = jnp.dot(lhs, matrix(b, 1, slots), preferred_element_type=jnp.float32)
                dst[pl.ds(2 * b, 2), :] = four_sum(y, bs)[0:2] + partial[pl.ds(2 * b, 2), :]
            return carry

        lax.fori_loop(0, rows // UNROLL, some, 0)

    ahead(ext_a, 0)
    keep(ext_a, 0)

    def pair(i, carry):
        for copy in field_copies(ext_a, 0):
            copy.wait()
        advance(ext_a, ext_b)
        for copy in field_copies(ext_b, 1):
            copy.start()
        ahead(ext_b, 2 * i + 1)
        keep(ext_b, 2 * i + 1)
        for copy in field_copies(ext_b, 1):
            copy.wait()
        advance(ext_b, ext_a)

        @pl.when(i < depth // 2 - 1)
        def _():
            for copy in field_copies(ext_a, 0):
                copy.start()
            ahead(ext_a, 2 * i + 2)

        keep(ext_a, 2 * i + 2)
        return carry

    lax.fori_loop(0, depth // 2, pair, 0)

    basis_copy = pltpu.make_async_copy(out, basis_hbm, out_sem.at[0])
    basis_copy.start()

    highs, lows = [], []
    for b in range(rows):
        high, low = split(fields[b])
        highs.append(high)
        lows.append(low)
    both = jnp.concatenate(
        [jnp.concatenate(highs, axis=1), jnp.concatenate(lows, axis=1)], axis=0
    )
    prod = lax.dot_general(
        both, both, (((1,), (1,)), ((), ())), preferred_element_type=jnp.float32
    )
    gram = (prod[GROWS:, GROWS:] + prod[GROWS:, :GROWS]) + (
        prod[:GROWS, GROWS:] + prod[:GROWS, :GROWS]
    )
    gram_mine[0] = jnp.zeros((8, bs), jnp.float32)
    for i in range(GROWS // 8):
        gram_mine[0, :, 32 * i : 32 * i + GROWS] = gram[8 * i : 8 * i + 8]

    phases = (
        (peers_a, COLUMN, w, gram_in_a, 0),
        (peers_b, n_x * n_group, g * n_x + x, gram_in_b, COLUMN),
    )
    total = None
    for number, (peers, count, mine, landing, first) in enumerate(phases):
        copies = [
            pltpu.make_async_remote_copy(
                src_ref=gram_mine.at[number],
                dst_ref=landing.at[mine],
                send_sem=gram_send.at[first + j],
                recv_sem=gram_recv.at[first + j],
                device_id=peer,
                device_id_type=MESH,
            )
            for j, peer in enumerate(peers)
        ]
        for copy in copies:
            copy.start()
        landing[mine] = gram_mine[number]
        for copy in copies:
            copy.wait()
        total = landing[0]
        for i in range(1, count):
            total = total + landing[i]
        if number < 1:
            gram_mine[number + 1] = total
    total = total * (1.0 / (rows * bs * n_group * n_dom))
    gram_out[...] = jnp.zeros((GROWS, bs), jnp.float32)
    for i in range(GROWS // 8):
        gram_out[8 * i : 8 * i + 8, 0:GROWS] = total[:, 32 * i : 32 * i + GROWS]
    gram_copy = pltpu.make_async_copy(gram_out, gram_hbm, out_sem.at[1])
    gram_copy.start()
    gram_copy.wait()
    basis_copy.wait()


def per_device(n_group, n_dom, p_start, r_start, diag_shift, shifts, block_values, block_cols, live_slots, needed):
    rows, bs = p_start.shape
    slots = block_cols.shape[1]
    halo = needed.shape[2]
    depth = shifts.shape[0]
    ncols = 2 * depth + 1
    f32 = jnp.float32
    hbm = pl.BlockSpec(memory_space=pl.ANY)
    smem = pl.BlockSpec(memory_space=pltpu.SMEM)
    dma = pltpu.SemaphoreType.DMA
    peers_b = n_group * n_dom // COLUMN
    basis, gram = pl.pallas_call(
        functools.partial(kernel, rows, slots, bs, halo, depth, n_group, n_dom),
        out_shape=(
            jax.ShapeDtypeStruct((ncols, rows, bs), f32),
            jax.ShapeDtypeStruct((GROWS, bs), f32),
        ),
        in_specs=[hbm, hbm, hbm, smem, hbm, smem, smem, smem],
        out_specs=(hbm, hbm),
        scratch_shapes=[
            pltpu.VMEM((rows, slots, bs, bs), f32),
            pltpu.VMEM((rows, 2, slots * bs, bs), jnp.bfloat16),
            pltpu.VMEM((10 * rows + 16, bs), f32),
            pltpu.VMEM((10 * rows + 16, bs), f32),
            pltpu.VMEM((rows, GROWS, bs), f32),
            pltpu.VMEM((ncols, rows, bs), f32),
            pltpu.VMEM((2, rows, bs), f32),
            pltpu.VMEM((rows, bs), f32),
            pltpu.SMEM((rows * slots,), jnp.int32),
            pltpu.VMEM((2 * rows, bs), f32),
            pltpu.VMEM((2, 8, bs), f32),
            pltpu.VMEM((COLUMN, 8, bs), f32),
            pltpu.VMEM((peers_b, 8, bs), f32),
            pltpu.VMEM((GROWS, bs), f32),
            dma((rows,)),
            dma((3,)),
            dma((2,)),
            dma((8,)),
            dma((8,)),
            dma((COLUMN + peers_b,)),
            dma((COLUMN + peers_b,)),
        ],
        compiler_params=pltpu.CompilerParams(
            collective_id=0, has_side_effects=True, vmem_limit_bytes=60 * 1024 * 1024
        ),
    )(p_start, r_start, diag_shift, shifts, block_values, block_cols.T, live_slots, needed)
    return basis, gram[:ncols, :ncols]


def solution(mesh):
    both = ("group", "dom")
    in_specs = (
        P(both, None),
        P(both, None),
        P(both, None),
        P(),
        P(both, None, None, None),
        P(both, None),
        P(both),
        P(both, None, None),
    )
    return jax.shard_map(
        functools.partial(per_device, mesh.shape["group"], mesh.shape["dom"]),
        mesh=mesh,
        in_specs=in_specs,
        out_specs=(P(None, both, None), P()),
        check_vma=False,
    )
```

time: 82.3 us -> 68.5 us (0.83)
  Pallas kernels: 76.1 us -> 64.5 us
  local copies, waits for them, and re-layouts: 4.36 us -> 2.99 us
    pallas_call x1, Pallas kernels: 76.1 us -> 64.5 us  [per_device(): pl.pallas_call(functools.partial(kernel, rows, slots, bs, halo, depth, n_...]
    unnamed x3 -> x2, local copies, waits for them, and re-layouts: 4.36 us -> 2.99 us
where the time goes in v1:
time: 68.5 us; the launch traced here: 68.1 us
  Pallas kernels  64.5 us (94%)
  local copies, waits for them, and re-layouts  2.99 us (4%)
    pallas_call x1, Pallas kernels, per_device(): pl.pallas_call(functools.partial(kernel, rows, slots, bs, halo, depth, n_...  64.5 us
    unnamed x2, local copies, waits for them, and re-layouts  2.99 us

profile of v1, /device:TPU:1, one launch (start us, length us, event | category | flops | bytes accessed | tf_op | source)
XLA Modules:
  0.0 68.1 jit_solution(2109729782057811935)
XLA Ops:
  0.6 64.5 %shard_map.95 = (f32[17,32,128]{2,1,0:T(8,128)}, f32[24,128]{1,0:T(8,128)}) custom-call(f32[32,128]{1,0:T(8,128)} %p_hbm.1, f32[32,128]{1,0:T(8,128)} %r_hbm.1, f32[32,128]{1,0:T(8,128)} %diag_hbm.1, f32[8]{0:T(128)} %shifts.1, f32[32,6,128,128]{3,2,1,0:T(8,128)} %values_hbm.1, s32[6,32]{1,0:T(8,128)} %bitcast.3, s32[32]{0:T(128)} %live.1, s32[1,4,16]{2,1,0:T(4,128)} %needed.1), custom_call_target="tpu_custom_call" | custom-call | tf_op jit(solution)/shard_map/pallas_call | solution.py:259
  65.1 1.7 %copy.12 = f32[17,32,128]{2,1,0:T(8,128)} copy(f32[17,32,128]{2,1,0:T(8,128)} %get-tuple-element.8) | data formatting | bytes 557056
  66.8 1.3 %copy.13 = f32[17,17]{1,0:T(8,128)} copy(f32[17,17]{1,0:T(8,128)} %bitcast.2) | data formatting | bytes 2312

commit v2 on v1

--- a/solution.py
+++ b/solution.py
@@ -30,11 +30,11 @@
 
 def kernel(
     rows, slots, bs, halo, depth, n_group, n_dom,
-    p_hbm, r_hbm, diag_hbm, shifts, values_hbm, cols, live, needed,
-    basis_hbm, gram_hbm,
-    stage, weights, ext_a, ext_b, fields, out, start, diag, index, partial,
-    gram_mine, gram_in_a, gram_in_b, gram_out,
-    value_sem, small_sem, out_sem, send_sem, recv_sem, gram_send, gram_recv,
+    p_hbm, r_hbm, diag_hbm, shifts_hbm, values_hbm, cols_hbm, live_hbm, needed_hbm,
+    out, gram_out,
+    shifts, cols, live, needed, stage, weights, ext_a, ext_b, fields, start, diag, index, partial,
+    gram_mine, gram_in_a, gram_in_b,
+    value_sem, small_sem, send_sem, recv_sem, gram_send, gram_recv,
 ):
     g = lax.axis_index("group")
     m = lax.axis_index("dom")
@@ -47,6 +47,10 @@
         pltpu.make_async_copy(p_hbm, start.at[0], small_sem.at[0]),
         pltpu.make_async_copy(r_hbm, start.at[1], small_sem.at[1]),
         pltpu.make_async_copy(diag_hbm, diag, small_sem.at[2]),
+        pltpu.make_async_copy(cols_hbm, cols, small_sem.at[3]),
+        pltpu.make_async_copy(live_hbm, live, small_sem.at[4]),
+        pltpu.make_async_copy(needed_hbm, needed, small_sem.at[5]),
+        pltpu.make_async_copy(shifts_hbm, shifts, small_sem.at[6]),
     ]
     for copy in small:
         copy.start()
@@ -61,10 +65,24 @@
     peers_b = [
         ((g + j // n_x) % n_group, (x + j) % n_x * COLUMN + w) for j in range(1, n_x * n_group)
     ]
-    greeted = list(neighbours[:2]) + peers_a + peers_b
+    before, after = m > 0, m < n_dom - 1
+
+    def where_there(k, act):
+        if k < 2:
+            pl.when((before, after)[k])(act)
+        else:
+            act()
+
     barrier = pltpu.get_barrier_semaphore()
-    for peer in greeted:
+
+    def greet(peer):
         pl.semaphore_signal(barrier, inc=1, device_id=peer, device_id_type=MESH)
+
+    for k in range(2):
+        where_there(k, functools.partial(greet, neighbours[k]))
+    for peer in peers_a + peers_b:
+        greet(peer)
+    greetings = len(peers_a + peers_b) + before.astype(jnp.int32) + after.astype(jnp.int32)
 
     def value_copy(b):
         return pltpu.make_async_copy(values_hbm.at[b], stage.at[b], value_sem.at[b])
@@ -83,18 +101,25 @@
     ext_a[pl.ds(1, rows, stride=2), :] = start[1]
     fields[...] = jnp.zeros(fields.shape, jnp.float32)
 
-    def field_copies(ext, parity):
-        return [
-            pltpu.make_async_remote_copy(
-                src_ref=ext.at[0:width],
-                dst_ref=ext.at[(1 + (k ^ 1)) * width : (2 + (k ^ 1)) * width],
-                send_sem=send_sem.at[4 * parity + k],
-                recv_sem=recv_sem.at[4 * parity + (k ^ 1)],
-                device_id=neighbours[k],
-                device_id_type=MESH,
-            )
-            for k in range(4)
-        ]
+    def field_copy(ext, parity, k, landing):
+        return pltpu.make_async_remote_copy(
+            src_ref=ext.at[0:width],
+            dst_ref=ext.at[(1 + landing) * width : (2 + landing) * width],
+            send_sem=send_sem.at[4 * parity + k],
+            recv_sem=recv_sem.at[4 * parity + landing],
+            device_id=neighbours[k],
+            device_id_type=MESH,
+        )
+
+    def send_field(ext, parity):
+        for k in range(4):
+            where_there(k, field_copy(ext, parity, k, k ^ 1).start)
+
+    def await_field(ext, parity):
+        for k in range(4):
+            where_there(k, field_copy(ext, parity, k, k).wait_recv)
+        for k in range(4):
+            where_there(k, field_copy(ext, parity, k, k ^ 1).wait_send)
 
     def prepare(b, carry):
         value_copy(b).wait()
@@ -112,9 +137,8 @@
         return carry
 
     lax.fori_loop(0, rows // 2, prepare, 0)
-    pl.semaphore_wait(barrier, len(greeted))
-    for copy in field_copies(ext_a, 0):
-        copy.start()
+    pl.semaphore_wait(barrier, greetings)
+    send_field(ext_a, 0)
     lax.fori_loop(rows // 2, rows, prepare, 0)
 
     def matrix(b, first, last):
@@ -165,30 +189,23 @@
     keep(ext_a, 0)
 
     def pair(i, carry):
-        for copy in field_copies(ext_a, 0):
-            copy.wait()
+        await_field(ext_a, 0)
         advance(ext_a, ext_b)
-        for copy in field_copies(ext_b, 1):
-            copy.start()
+        send_field(ext_b, 1)
         ahead(ext_b, 2 * i + 1)
         keep(ext_b, 2 * i + 1)
-        for copy in field_copies(ext_b, 1):
-            copy.wait()
+        await_field(ext_b, 1)
         advance(ext_b, ext_a)
 
         @pl.when(i < depth // 2 - 1)
         def _():
-            for copy in field_copies(ext_a, 0):
-                copy.start()
+            send_field(ext_a, 0)
             ahead(ext_a, 2 * i + 2)
 
         keep(ext_a, 2 * i + 2)
         return carry
 
     lax.fori_loop(0, depth // 2, pair, 0)
-
-    basis_copy = pltpu.make_async_copy(out, basis_hbm, out_sem.at[0])
-    basis_copy.start()
 
     highs, lows = [], []
     for b in range(rows):
@@ -236,13 +253,21 @@
         if number < 1:
             gram_mine[number + 1] = total
     total = total * (1.0 / (rows * bs * n_group * n_dom))
-    gram_out[...] = jnp.zeros((GROWS, bs), jnp.float32)
-    for i in range(GROWS // 8):
-        gram_out[8 * i : 8 * i + 8, 0:GROWS] = total[:, 32 * i : 32 * i + GROWS]
-    gram_copy = pltpu.make_async_copy(gram_out, gram_hbm, out_sem.at[1])
-    gram_copy.start()
-    gram_copy.wait()
-    basis_copy.wait()
+    ncols = 2 * depth + 1
+    for i in range(0, ncols, 8):
+        some = min(8, ncols - i)
+        gram_out[i : i + some, :] = total[0:some, 4 * i : 4 * i + ncols]
+
+
+def deliver(basis, gram, basis_out, gram_out, sems):
+    copies = [
+        pltpu.make_async_copy(basis, basis_out, sems.at[0]),
+        pltpu.make_async_copy(gram, gram_out, sems.at[1]),
+    ]
+    for copy in copies:
+        copy.start()
+    for copy in copies:
+        copy.wait()
 
 
 def per_device(n_group, n_dom, p_start, r_start, diag_shift, shifts, block_values, block_cols, live_slots, needed):
@@ -252,25 +277,29 @@
     depth = shifts.shape[0]
     ncols = 2 * depth + 1
     f32 = jnp.float32
-    hbm = pl.BlockSpec(memory_space=pl.ANY)
-    smem = pl.BlockSpec(memory_space=pltpu.SMEM)
+    hbm = pl.BlockSpec(memory_space=pltpu.HBM)
     dma = pltpu.SemaphoreType.DMA
     peers_b = n_group * n_dom // COLUMN
+    vmem = pl.BlockSpec(memory_space=pltpu.VMEM)
+    results = (
+        jax.ShapeDtypeStruct((ncols, rows, bs), f32),
+        jax.ShapeDtypeStruct((ncols, ncols), f32),
+    )
     basis, gram = pl.pallas_call(
         functools.partial(kernel, rows, slots, bs, halo, depth, n_group, n_dom),
-        out_shape=(
-            jax.ShapeDtypeStruct((ncols, rows, bs), f32),
-            jax.ShapeDtypeStruct((GROWS, bs), f32),
-        ),
-        in_specs=[hbm, hbm, hbm, smem, hbm, smem, smem, smem],
-        out_specs=(hbm, hbm),
+        out_shape=tuple(pltpu.VMEM(r.shape, r.dtype) for r in results),
+        in_specs=[hbm] * 8,
+        out_specs=(vmem, vmem),
         scratch_shapes=[
+            pltpu.SMEM((depth,), f32),
+            pltpu.SMEM((slots, rows), jnp.int32),
+            pltpu.SMEM((rows,), jnp.int32),
+            pltpu.SMEM((1, 4, halo), jnp.int32),
             pltpu.VMEM((rows, slots, bs, bs), f32),
             pltpu.VMEM((rows, 2, slots * bs, bs), jnp.bfloat16),
             pltpu.VMEM((10 * rows + 16, bs), f32),
             pltpu.VMEM((10 * rows + 16, bs), f32),
             pltpu.VMEM((rows, GROWS, bs), f32),
-            pltpu.VMEM((ncols, rows, bs), f32),
             pltpu.VMEM((2, rows, bs), f32),
             pltpu.VMEM((rows, bs), f32),
             pltpu.SMEM((rows * slots,), jnp.int32),
@@ -278,10 +307,8 @@
             pltpu.VMEM((2, 8, bs), f32),
             pltpu.VMEM((COLUMN, 8, bs), f32),
             pltpu.VMEM((peers_b, 8, bs), f32),
-            pltpu.VMEM((GROWS, bs), f32),
             dma((rows,)),
-            dma((3,)),
-            dma((2,)),
+            dma((7,)),
             dma((8,)),
             dma((8,)),
             dma((COLUMN + peers_b,)),
@@ -291,7 +318,14 @@
             collective_id=0, has_side_effects=True, vmem_limit_bytes=60 * 1024 * 1024
         ),
     )(p_start, r_start, diag_shift, shifts, block_values, block_cols.T, live_slots, needed)
-    return basis, gram[:ncols, :ncols]
+    return pl.pallas_call(
+        deliver,
+        out_shape=results,
+        in_specs=[vmem, vmem],
+        out_specs=(hbm, hbm),
+        scratch_shapes=[dma((2,))],
+        compiler_params=pltpu.CompilerParams(vmem_limit_bytes=4 * 1024 * 1024),
+    )(basis, gram)
 
 
 def solution(mesh):

time: 68.5 us -> 60.8 us (0.89)
  Pallas kernels: 64.5 us -> 59.9 us
  local copies, waits for them, and re-layouts: 2.99 us -> 0 us
    pallas_call x1, Pallas kernels: 64.5 us -> 59.2 us  [per_device(): pl.pallas_call(functools.partial(kernel, rows, slots, bs, halo, depth, n_...]
    unnamed x2 -> x0, local copies, waits for them, and re-layouts: 2.99 us -> none
    pallas_call x0 -> x1, Pallas kernels: none -> 0.73 us  [per_device(): pl.pallas_call(deliver, out_shape=results, in_specs=[vmem, vmem], out_spe...]
where the time goes in v2:
time: 60.8 us; the launch traced here: 60.6 us
  Pallas kernels  59.9 us (99%)
  between operations  0.64 us (1%)
    pallas_call x1, Pallas kernels, per_device(): pl.pallas_call(functools.partial(kernel, rows, slots, bs, halo, depth, n_...  59.2 us

profile of v2, /device:TPU:1, one launch (start us, length us, event | category | flops | bytes accessed | tf_op | source)
XLA Modules:
  0.0 60.6 jit_solution(16232504016051676769)
XLA Ops:
  0.6 59.2 %shard_map.95 = (f32[17,32,128]{2,1,0:T(8,128)S(1)}, f32[17,17]{1,0:T(8,128)S(1)}) custom-call(f32[32,128]{1,0:T(8,128)} %p_hbm.1, f32[32,128]{1,0:T(8,128)} %r_hbm.1, f32[32,128]{1,0:T(8,128)} %diag_hbm.1, f32[8]{0:T(128)} %shifts_hbm.1, f32[32,6,128,128]{3,2,1,0:T(8,128)} %values_hbm.1, s32[6,32]{1,0:T(8,128)} %bitcast.1, s32[32]{0:T(128)} %live_hbm.1, ...), custom_call_target="tpu_custom_call" | custom-call | tf_op jit(solution)/shard_map/pallas_call | solution.py:288
  59.9 0.7 %shard_map.96 = (f32[17,32,128]{2,1,0:T(8,128)}, f32[17,17]{1,0:T(8,128)}) custom-call(f32[17,32,128]{2,1,0:T(8,128)S(1)} %get-tuple-element.4.basis, f32[17,17]{1,0:T(8,128)S(1)} %get-tuple-element.5.gram), custom_call_target="tpu_custom_call" | custom-call | tf_op jit(solution)/shard_map/pallas_call | solution.py:321

commit v3 on v2

--- a/solution.py
+++ b/solution.py
@@ -9,6 +9,8 @@
 
 MESH = pl.DeviceIdType.MESH
 UNROLL = 32
+TOGETHER = 4
+EARLY = 8
 GROWS = 24
 COLUMN = 8
 
@@ -33,8 +35,8 @@
     p_hbm, r_hbm, diag_hbm, shifts_hbm, values_hbm, cols_hbm, live_hbm, needed_hbm,
     out, gram_out,
     shifts, cols, live, needed, stage, weights, ext_a, ext_b, fields, start, diag, index, partial,
-    gram_mine, gram_in_a, gram_in_b,
-    value_sem, small_sem, send_sem, recv_sem, gram_send, gram_recv,
+    gram_mine, gram_in_a, gram_in_b, row_mine, row_in,
+    value_sem, small_sem, send_sem, recv_sem, gram_send, gram_recv, row_send, row_recv,
 ):
     g = lax.axis_index("group")
     m = lax.axis_index("dom")
@@ -121,8 +123,7 @@
         for k in range(4):
             where_there(k, field_copy(ext, parity, k, k ^ 1).wait_send)
 
-    def prepare(b, carry):
-        value_copy(b).wait()
+    def prepare_one(b):
         for s in range(slots):
             high, low = split(stage[b, s].T)
             weights[b, 0, s * bs : (s + 1) * bs, :] = high
@@ -134,12 +135,18 @@
             k, h = far // halo, far % halo
             spot = jnp.where(c < rows, c, (1 + k) * rows + needed[0, k, h])
             index[b * slots + s] = jnp.where(s < used, 2 * spot, nothing)
+
+    def prepare(i, carry):
+        for u in range(TOGETHER):
+            value_copy(i * TOGETHER + u).wait()
+        for u in range(TOGETHER):
+            prepare_one(i * TOGETHER + u)
         return carry
 
-    lax.fori_loop(0, rows // 2, prepare, 0)
+    lax.fori_loop(0, EARLY // TOGETHER, prepare, 0)
     pl.semaphore_wait(barrier, greetings)
     send_field(ext_a, 0)
-    lax.fori_loop(rows // 2, rows, prepare, 0)
+    lax.fori_loop(EARLY // TOGETHER, rows // TOGETHER, prepare, 0)
 
     def matrix(b, first, last):
         span = slice(first * bs, last * bs)
@@ -185,53 +192,33 @@
 
         lax.fori_loop(0, rows // UNROLL, some, 0)
 
-    ahead(ext_a, 0)
-    keep(ext_a, 0)
-
-    def pair(i, carry):
-        await_field(ext_a, 0)
-        advance(ext_a, ext_b)
-        send_field(ext_b, 1)
-        ahead(ext_b, 2 * i + 1)
-        keep(ext_b, 2 * i + 1)
-        await_field(ext_b, 1)
-        advance(ext_b, ext_a)
-
-        @pl.when(i < depth // 2 - 1)
-        def _():
-            send_field(ext_a, 0)
-            ahead(ext_a, 2 * i + 2)
-
-        keep(ext_a, 2 * i + 2)
-        return carry
-
-    lax.fori_loop(0, depth // 2, pair, 0)
-
-    highs, lows = [], []
-    for b in range(rows):
-        high, low = split(fields[b])
-        highs.append(high)
-        lows.append(low)
-    both = jnp.concatenate(
-        [jnp.concatenate(highs, axis=1), jnp.concatenate(lows, axis=1)], axis=0
-    )
-    prod = lax.dot_general(
-        both, both, (((1,), (1,)), ((), ())), preferred_element_type=jnp.float32
-    )
-    gram = (prod[GROWS:, GROWS:] + prod[GROWS:, :GROWS]) + (
-        prod[:GROWS, GROWS:] + prod[:GROWS, :GROWS]
-    )
-    gram_mine[0] = jnp.zeros((8, bs), jnp.float32)
-    for i in range(GROWS // 8):
-        gram_mine[0, :, 32 * i : 32 * i + GROWS] = gram[8 * i : 8 * i + 8]
-
-    phases = (
-        (peers_a, COLUMN, w, gram_in_a, 0),
-        (peers_b, n_x * n_group, g * n_x + x, gram_in_b, COLUMN),
-    )
-    total = None
-    for number, (peers, count, mine, landing, first) in enumerate(phases):
-        copies = [
+    def gram_part():
+        highs, lows = [], []
+        for b in range(rows):
+            high, low = split(fields[b])
+            highs.append(high)
+            lows.append(low)
+        both = jnp.concatenate(
+            [jnp.concatenate(highs, axis=1), jnp.concatenate(lows, axis=1)], axis=0
+        )
+        prod = lax.dot_general(
+            both, both, (((1,), (1,)), ((), ())), preferred_element_type=jnp.float32
+        )
+        gram = (prod[GROWS:, GROWS:] + prod[GROWS:, :GROWS]) + (
+            prod[:GROWS, GROWS:] + prod[:GROWS, :GROWS]
+        )
+        gram_mine[0] = jnp.zeros((8, bs), jnp.float32)
+        for i in range(GROWS // 8):
+            gram_mine[0, :, 32 * i : 32 * i + GROWS] = gram[8 * i : 8 * i + 8]
+
+    rounds = (
+        (peers_a, w, gram_in_a, 0),
+        (peers_b, g * n_x + x, gram_in_b, COLUMN),
+    )
+
+    def round_copies(number):
+        peers, mine, landing, first = rounds[number]
+        return [
             pltpu.make_async_remote_copy(
                 src_ref=gram_mine.at[number],
                 dst_ref=landing.at[mine],
@@ -242,21 +229,112 @@
             )
             for j, peer in enumerate(peers)
         ]
-        for copy in copies:
+
+    def start_round(number):
+        _, mine, landing, _ = rounds[number]
+        for copy in round_copies(number):
             copy.start()
         landing[mine] = gram_mine[number]
-        for copy in copies:
+
+    def end_round(number):
+        peers, _, landing, _ = rounds[number]
+        for copy in round_copies(number):
             copy.wait()
         total = landing[0]
-        for i in range(1, count):
+        for i in range(1, len(peers) + 1):
             total = total + landing[i]
-        if number < 1:
-            gram_mine[number + 1] = total
-    total = total * (1.0 / (rows * bs * n_group * n_dom))
+        return total
+
+    ahead(ext_a, 0)
+    keep(ext_a, 0)
+
+    def pair(i, carry):
+        await_field(ext_a, 0)
+        advance(ext_a, ext_b)
+        send_field(ext_b, 1)
+        ahead(ext_b, 2 * i + 1)
+        keep(ext_b, 2 * i + 1)
+
+        @pl.when(i == depth // 2 - 1)
+        def _():
+            gram_part()
+            start_round(0)
+
+        await_field(ext_b, 1)
+        advance(ext_b, ext_a)
+
+        @pl.when(i < depth // 2 - 1)
+        def _():
+            send_field(ext_a, 0)
+            ahead(ext_a, 2 * i + 2)
+
+        keep(ext_a, 2 * i + 2)
+        return carry
+
+    lax.fori_loop(0, depth // 2, pair, 0)
+
+    last = jnp.zeros((GROWS, bs), jnp.float32)
+    for b in range(rows):
+        last = last + fields[b] * ext_a[2 * b : 2 * b + 1, :]
+    row_mine[...] = jnp.zeros((1, bs), jnp.float32)
+    row_mine[:, 0:GROWS] = jnp.sum(last.T, axis=0, keepdims=True)
+    count = n_group * n_dom
+    me = g * n_dom + m
+
+    def hops(offset, size):
+        return min(offset, size - offset)
+
+    offsets = sorted(
+        ((dg, dx) for dg in range(n_group) for dx in range(n_x)),
+        key=lambda o: -(hops(o[0], n_group) + hops(o[1], n_x)),
+    )
+    for dg, dx in offsets:
+
+        def send_row(j, carry, to_g=(g + dg) % n_group, to_x=(x + dx) % n_x):
+            pltpu.make_async_remote_copy(
+                src_ref=row_mine,
+                dst_ref=row_in.at[me],
+                send_sem=row_send.at[0],
+                recv_sem=row_recv.at[0],
+                device_id=(to_g, to_x * COLUMN + (w + j) % COLUMN),
+                device_id_type=MESH,
+            ).start()
+            return carry
+
+        for j in range(0 if dg or dx else 1, COLUMN):
+            send_row(j, 0)
+    row_in[me] = row_mine[...]
+
+    gram_mine[1] = end_round(0)
+    start_round(1)
+    total = end_round(1)
+
+    rows_sent = pltpu.make_async_remote_copy(
+        src_ref=row_in.at[0 : count - 1],
+        dst_ref=row_in.at[0 : count - 1],
+        send_sem=row_send.at[0],
+        recv_sem=row_recv.at[0],
+        device_id=neighbours[3],
+        device_id_type=MESH,
+    )
+    rows_sent.wait_recv()
+    rows_sent.wait_send()
+    row = row_in[0]
+    for i in range(1, count):
+        row = row + row_in[i]
+
+    scale = 1.0 / (rows * bs * count)
     ncols = 2 * depth + 1
+    across = jnp.broadcast_to(row, (bs, bs))
+    down = across.T
     for i in range(0, ncols, 8):
         some = min(8, ncols - i)
-        gram_out[i : i + some, :] = total[0:some, 4 * i : 4 * i + ncols]
+        part = total[0:some, 4 * i : 4 * i + ncols]
+        r = i + lax.broadcasted_iota(jnp.int32, (some, ncols), 0)
+        c = lax.broadcasted_iota(jnp.int32, (some, ncols), 1)
+        part = jnp.where(c == depth, down[i : i + some, 0:ncols], part)
+        part = jnp.where(r == depth, across[i : i + some, 0:ncols], part)
+        gram_out[i : i + some, :] = part * scale
 
 
 def deliver(basis, gram, basis_out, gram_out, sems):
@@ -307,12 +385,16 @@
             pltpu.VMEM((2, 8, bs), f32),
             pltpu.VMEM((COLUMN, 8, bs), f32),
             pltpu.VMEM((peers_b, 8, bs), f32),
+            pltpu.VMEM((1, bs), f32),
+            pltpu.VMEM((n_group * n_dom, 1, bs), f32),
             dma((rows,)),
             dma((7,)),
             dma((8,)),
             dma((8,)),
             dma((COLUMN + peers_b,)),
             dma((COLUMN + peers_b,)),
+            dma((1,)),
+            dma((1,)),
         ],
         compiler_params=pltpu.CompilerParams(
             collective_id=0, has_side_effects=True, vmem_limit_bytes=60 * 1024 * 1024

time: 60.8 us -> 57.8 us (0.951)
  Pallas kernels: 59.9 us -> 57 us
    pallas_call x1, Pallas kernels: 59.2 us -> 56.3 us  [per_device(): pl.pallas_call(functools.partial(kernel, rows, slots, bs, halo, depth, n_...]
where the time goes in v3:
time: 57.8 us; the launch traced here: 57.6 us
  Pallas kernels  57 us (99%)
  between operations  0.64 us (1%)
    pallas_call x1, Pallas kernels, per_device(): pl.pallas_call(functools.partial(kernel, rows, slots, bs, halo, depth, n_...  56.3 us

profile of v3, /device:TPU:1, one launch (start us, length us, event | category | flops | bytes accessed | tf_op | source)
XLA Modules:
  0.0 57.6 jit_solution(4441890550060401684)
XLA Ops:
  0.6 56.3 %shard_map.95 = (f32[17,32,128]{2,1,0:T(8,128)S(1)}, f32[17,17]{1,0:T(8,128)S(1)}) custom-call(f32[32,128]{1,0:T(8,128)} %p_hbm.1, f32[32,128]{1,0:T(8,128)} %r_hbm.1, f32[32,128]{1,0:T(8,128)} %diag_hbm.1, f32[8]{0:T(128)} %shifts_hbm.1, f32[32,6,128,128]{3,2,1,0:T(8,128)} %values_hbm.1, s32[6,32]{1,0:T(8,128)} %bitcast.1, s32[32]{0:T(128)} %live_hbm.1, ...), custom_call_target="tpu_custom_call" | custom-call | tf_op jit(solution)/shard_map/pallas_call | solution.py:366
  56.9 0.7 %shard_map.96 = (f32[17,32,128]{2,1,0:T(8,128)}, f32[17,17]{1,0:T(8,128)}) custom-call(f32[17,32,128]{2,1,0:T(8,128)S(1)} %get-tuple-element.4.basis, f32[17,17]{1,0:T(8,128)S(1)} %get-tuple-element.5.gram), custom_call_target="tpu_custom_call" | custom-call | tf_op jit(solution)/shard_map/pallas_call | solution.py:403

commit v4 on v3

--- a/solution.py
+++ b/solution.py
@@ -34,9 +34,9 @@
     rows, slots, bs, halo, depth, n_group, n_dom,
     p_hbm, r_hbm, diag_hbm, shifts_hbm, values_hbm, cols_hbm, live_hbm, needed_hbm,
     out, gram_out,
-    shifts, cols, live, needed, stage, weights, ext_a, ext_b, fields, start, diag, index, partial,
+    shifts, cols, live, needed, wanted, stage, weights, ext_a, ext_b, fields, start, diag, index, partial, own, parcel, lists, lists_in,
     gram_mine, gram_in_a, gram_in_b, row_mine, row_in,
-    value_sem, small_sem, send_sem, recv_sem, gram_send, gram_recv, row_send, row_recv,
+    value_sem, small_sem, send_sem, recv_sem, gram_send, gram_recv, row_send, row_recv, list_send, list_recv,
 ):
     g = lax.axis_index("group")
     m = lax.axis_index("dom")
@@ -53,10 +53,8 @@
         pltpu.make_async_copy(live_hbm, live, small_sem.at[4]),
         pltpu.make_async_copy(needed_hbm, needed, small_sem.at[5]),
         pltpu.make_async_copy(shifts_hbm, shifts, small_sem.at[6]),
+        pltpu.make_async_copy(needed_hbm, lists, small_sem.at[7]),
     ]
-    for copy in small:
-        copy.start()
-
     neighbours = (
         (g, (m + n_dom - 1) % n_dom),
         (g, (m + 1) % n_dom),
@@ -67,6 +65,16 @@
     peers_b = [
         ((g + j // n_x) % n_group, (x + j) % n_x * COLUMN + w) for j in range(1, n_x * n_group)
     ]
+    def hops(offset, size):
+        return min(offset, size - offset)
+
+    sorted_b = [
+        peers_b[j - 1]
+        for j in sorted(
+            range(1, n_x * n_group), key=lambda j: -(hops(j // n_x, n_group) + hops(j % n_x, n_x))
+        )
+    ]
+
     before, after = m > 0, m < n_dom - 1
 
     def where_there(k, act):
@@ -75,15 +83,18 @@
         else:
             act()
 
+    lists_in[...] = jnp.zeros(lists_in.shape, jnp.int32)
     barrier = pltpu.get_barrier_semaphore()
 
     def greet(peer):
         pl.semaphore_signal(barrier, inc=1, device_id=peer, device_id_type=MESH)
 
+    for peer in sorted_b + peers_a:
+        greet(peer)
     for k in range(2):
         where_there(k, functools.partial(greet, neighbours[k]))
-    for peer in peers_a + peers_b:
-        greet(peer)
+    for copy in small:
+        copy.start()
     greetings = len(peers_a + peers_b) + before.astype(jnp.int32) + after.astype(jnp.int32)
 
     def value_copy(b):
@@ -103,25 +114,56 @@
     ext_a[pl.ds(1, rows, stride=2), :] = start[1]
     fields[...] = jnp.zeros(fields.shape, jnp.float32)
 
+    def whole_copy(k, landing):
+        return pltpu.make_async_remote_copy(
+            src_ref=ext_a.at[0:width],
+            dst_ref=ext_a.at[(1 + landing) * width : (2 + landing) * width],
+            send_sem=send_sem.at[8 + k],
+            recv_sem=recv_sem.at[8 + landing],
+            device_id=neighbours[k],
+            device_id_type=MESH,
+        )
+
+    def list_copy(k, landing):
+        return pltpu.make_async_remote_copy(
+            src_ref=lists,
+            dst_ref=lists_in.at[landing : landing + 1],
+            send_sem=list_send.at[k],
+            recv_sem=list_recv.at[landing],
+            device_id=neighbours[k],
+            device_id_type=MESH,
+        )
+
     def field_copy(ext, parity, k, landing):
+        span = 2 * halo
         return pltpu.make_async_remote_copy(
-            src_ref=ext.at[0:width],
-            dst_ref=ext.at[(1 + landing) * width : (2 + landing) * width],
+            src_ref=parcel.at[k],
+            dst_ref=ext.at[width + landing * span : width + (1 + landing) * span],
             send_sem=send_sem.at[4 * parity + k],
             recv_sem=recv_sem.at[4 * parity + landing],
             device_id=neighbours[k],
             device_id_type=MESH,
         )
 
+    def send_all(copy_of):
+        for k in (2, 3, 0, 1):
+            where_there(k, copy_of(k, k ^ 1).start)
+
+    def await_all(copy_of):
+        for k in range(4):
+            where_there(k, copy_of(k, k).wait_recv)
+        for k in range(4):
+            where_there(k, copy_of(k, k ^ 1).wait_send)
+
     def send_field(ext, parity):
         for k in range(4):
-            where_there(k, field_copy(ext, parity, k, k ^ 1).start)
+            for h in range(halo):
+                block = wanted[k, k ^ 1, h]
+                parcel[k, 2 * h : 2 * h + 2, :] = own[pl.ds(2 * block, 2), :]
+        send_all(functools.partial(field_copy, ext, parity))
 
     def await_field(ext, parity):
-        for k in range(4):
-            where_there(k, field_copy(ext, parity, k, k).wait_recv)
-        for k in range(4):
-            where_there(k, field_copy(ext, parity, k, k ^ 1).wait_send)
+        await_all(functools.partial(field_copy, ext, parity))
 
     def prepare_one(b):
         for s in range(slots):
@@ -135,6 +177,7 @@
             k, h = far // halo, far % halo
             spot = jnp.where(c < rows, c, (1 + k) * rows + needed[0, k, h])
             index[b * slots + s] = jnp.where(s < used, 2 * spot, nothing)
+            index[(rows + b) * slots + s] = jnp.where(s < used, 2 * c, nothing)
 
     def prepare(i, carry):
         for u in range(TOGETHER):
@@ -145,7 +188,8 @@
 
     lax.fori_loop(0, EARLY // TOGETHER, prepare, 0)
     pl.semaphore_wait(barrier, greetings)
-    send_field(ext_a, 0)
+    send_all(whole_copy)
+    send_all(list_copy)
     lax.fori_loop(EARLY // TOGETHER, rows // TOGETHER, prepare, 0)
 
     def matrix(b, first, last):
@@ -175,19 +219,21 @@
                 near = four_sum(y, bs)[two] + (diag[b : b + 1, :] - theta) * own[two]
                 partial[2 * b : 2 * b + 2, :] = near
 
-    def advance(src, dst):
+    def advance(src, dst, table):
         def some(i, carry):
             for u in range(UNROLL):
                 b = i * UNROLL + u
                 lhs = jnp.concatenate(
                     [
-                        both_halves(src[pl.ds(index[b * slots + s], 8), :])
+                        both_halves(src[pl.ds(index[(table * rows + b) * slots + s], 8), :])
                         for s in range(1, slots)
                     ],
                     axis=1,
                 )
                 y = jnp.dot(lhs, matrix(b, 1, slots), preferred_element_type=jnp.float32)
-                dst[pl.ds(2 * b, 2), :] = four_sum(y, bs)[0:2] + partial[pl.ds(2 * b, 2), :]
+                new = four_sum(y, bs)[0:2] + partial[pl.ds(2 * b, 2), :]
+                dst[pl.ds(2 * b, 2), :] = new
+                own[pl.ds(2 * b, 2), :] = new
             return carry
 
         lax.fori_loop(0, rows // UNROLL, some, 0)
@@ -247,10 +293,21 @@
 
     ahead(ext_a, 0)
     keep(ext_a, 0)
+    await_all(list_copy)
+    fetch = pltpu.make_async_copy(lists_in, wanted, small_sem.at[0])
+    fetch.start()
+    fetch.wait()
 
     def pair(i, carry):
-        await_field(ext_a, 0)
-        advance(ext_a, ext_b)
+        @pl.when(i == 0)
+        def _():
+            await_all(whole_copy)
+
+        @pl.when(i > 0)
+        def _():
+            await_field(ext_a, 0)
+
+        advance(ext_a, ext_b, jnp.minimum(i, 1))
         send_field(ext_b, 1)
         ahead(ext_b, 2 * i + 1)
         keep(ext_b, 2 * i + 1)
@@ -261,7 +318,7 @@
             start_round(0)
 
         await_field(ext_b, 1)
-        advance(ext_b, ext_a)
+        advance(ext_b, ext_a, 1)
 
         @pl.when(i < depth // 2 - 1)
         def _():
@@ -280,9 +337,6 @@
     row_mine[:, 0:GROWS] = jnp.sum(last.T, axis=0, keepdims=True)
     count = n_group * n_dom
     me = g * n_dom + m
-
-    def hops(offset, size):
-        return min(offset, size - offset)
 
     offsets = sorted(
         ((dg, dx) for dg in range(n_group) for dx in range(n_x)),
@@ -319,9 +373,12 @@
     )
     rows_sent.wait_recv()
     rows_sent.wait_send()
-    row = row_in[0]
-    for i in range(1, count):
-        row = row + row_in[i]
+    sums = [row_in[i] for i in range(8)]
+    for i in range(8, count):
+        sums[i % 8] = sums[i % 8] + row_in[i]
+    while len(sums) > 1:
+        sums = [a + b for a, b in zip(sums[0::2], sums[1::2])]
+    row = sums[0]
 
     scale = 1.0 / (rows * bs * count)
     ncols = 2 * depth + 1
@@ -373,6 +430,7 @@
             pltpu.SMEM((slots, rows), jnp.int32),
             pltpu.SMEM((rows,), jnp.int32),
             pltpu.SMEM((1, 4, halo), jnp.int32),
+            pltpu.SMEM((4, 4, halo), jnp.int32),
             pltpu.VMEM((rows, slots, bs, bs), f32),
             pltpu.VMEM((rows, 2, slots * bs, bs), jnp.bfloat16),
             pltpu.VMEM((10 * rows + 16, bs), f32),
@@ -380,21 +438,27 @@
             pltpu.VMEM((rows, GROWS, bs), f32),
             pltpu.VMEM((2, rows, bs), f32),
             pltpu.VMEM((rows, bs), f32),
-            pltpu.SMEM((rows * slots,), jnp.int32),
+            pltpu.SMEM((2 * rows * slots,), jnp.int32),
             pltpu.VMEM((2 * rows, bs), f32),
+            pltpu.VMEM((2 * rows, bs), f32),
+            pltpu.VMEM((4, 2 * halo, bs), f32),
+            pltpu.VMEM((1, 4, halo), jnp.int32),
+            pltpu.VMEM((4, 4, halo), jnp.int32),
             pltpu.VMEM((2, 8, bs), f32),
             pltpu.VMEM((COLUMN, 8, bs), f32),
             pltpu.VMEM((peers_b, 8, bs), f32),
             pltpu.VMEM((1, bs), f32),
             pltpu.VMEM((n_group * n_dom, 1, bs), f32),
             dma((rows,)),
-            dma((7,)),
             dma((8,)),
-            dma((8,)),
+            dma((12,)),
+            dma((12,)),
             dma((COLUMN + peers_b,)),
             dma((COLUMN + peers_b,)),
             dma((1,)),
             dma((1,)),
+            dma((4,)),
+            dma((4,)),
         ],
         compiler_params=pltpu.CompilerParams(
             collective_id=0, has_side_effects=True, vmem_limit_bytes=60 * 1024 * 1024

time: 57.8 us -> 57.6 us (level)
  no operation moved by 1% of the time
where the time goes in v4:
time: 57.6 us; the launch traced here: 57.5 us
  Pallas kernels  56.8 us (99%)
  between operations  0.64 us (1%)
    pallas_call x1, Pallas kernels, per_device(): pl.pallas_call(functools.partial(kernel, rows, slots, bs, halo, depth, n_...  56.1 us

profile of v4, /device:TPU:1, one launch (start us, length us, event | category | flops | bytes accessed | tf_op | source)
XLA Modules:
  0.0 57.5 jit_solution(12240509829236172402)
XLA Ops:
  0.6 56.1 %shard_map.95 = (f32[17,32,128]{2,1,0:T(8,128)S(1)}, f32[17,17]{1,0:T(8,128)S(1)}) custom-call(f32[32,128]{1,0:T(8,128)} %p_hbm.1, f32[32,128]{1,0:T(8,128)} %r_hbm.1, f32[32,128]{1,0:T(8,128)} %diag_hbm.1, f32[8]{0:T(128)} %shifts_hbm.1, f32[32,6,128,128]{3,2,1,0:T(8,128)} %values_hbm.1, s32[6,32]{1,0:T(8,128)} %bitcast.1, s32[32]{0:T(128)} %live_hbm.1, ...), custom_call_target="tpu_custom_call" | custom-call | tf_op jit(solution)/shard_map/pallas_call | solution.py:423
  56.7 0.7 %shard_map.96 = (f32[17,32,128]{2,1,0:T(8,128)}, f32[17,17]{1,0:T(8,128)}) custom-call(f32[17,32,128]{2,1,0:T(8,128)S(1)} %get-tuple-element.4.basis, f32[17,17]{1,0:T(8,128)S(1)} %get-tuple-element.5.gram), custom_call_target="tpu_custom_call" | custom-call | tf_op jit(solution)/shard_map/pallas_call | solution.py:467

commit v5 on v4

--- a/solution.py
+++ b/solution.py
@@ -325,14 +325,20 @@
             send_field(ext_a, 0)
             ahead(ext_a, 2 * i + 2)
 
-        keep(ext_a, 2 * i + 2)
+            keep(ext_a, 2 * i + 2)
+
         return carry
 
     lax.fori_loop(0, depth // 2, pair, 0)
 
     last = jnp.zeros((GROWS, bs), jnp.float32)
+    square = jnp.zeros((1, bs), jnp.float32)
     for b in range(rows):
-        last = last + fields[b] * ext_a[2 * b : 2 * b + 1, :]
+        new = ext_a[2 * b : 2 * b + 1, :]
+        last = last + fields[b] * new
+        square = square + new * new
+    at = lax.broadcasted_iota(jnp.int32, (GROWS, bs), 0)
+    last = jnp.where(at == depth, square, last)
     row_mine[...] = jnp.zeros((1, bs), jnp.float32)
     row_mine[:, 0:GROWS] = jnp.sum(last.T, axis=0, keepdims=True)
     count = n_group * n_dom
@@ -358,6 +364,7 @@
         for j in range(0 if dg or dx else 1, COLUMN):
             send_row(j, 0)
     row_in[me] = row_mine[...]
+    out[depth] = ext_a[pl.ds(0, rows, stride=2), :]
 
     gram_mine[1] = end_round(0)
     start_round(1)

time: 57.6 us -> 57.6 us (level)
  no operation moved by 1% of the time
where the time goes in v5:
time: 57.6 us; the launch traced here: 57.4 us
  Pallas kernels  56.8 us (99%)
  between operations  0.64 us (1%)
    pallas_call x1, Pallas kernels, per_device(): pl.pallas_call(functools.partial(kernel, rows, slots, bs, halo, depth, n_...  56.1 us

profile of v5, /device:TPU:1, one launch (start us, length us, event | category | flops | bytes accessed | tf_op | source)
XLA Modules:
  0.0 57.4 jit_solution(3054922143660445710)
XLA Ops:
  0.6 56.1 %shard_map.95 = (f32[17,32,128]{2,1,0:T(8,128)S(1)}, f32[17,17]{1,0:T(8,128)S(1)}) custom-call(f32[32,128]{1,0:T(8,128)} %p_hbm.1, f32[32,128]{1,0:T(8,128)} %r_hbm.1, f32[32,128]{1,0:T(8,128)} %diag_hbm.1, f32[8]{0:T(128)} %shifts_hbm.1, f32[32,6,128,128]{3,2,1,0:T(8,128)} %values_hbm.1, s32[6,32]{1,0:T(8,128)} %bitcast.1, s32[32]{0:T(128)} %live_hbm.1, ...), custom_call_target="tpu_custom_call" | custom-call | tf_op jit(solution)/shard_map/pallas_call | solution.py:430
  56.7 0.7 %shard_map.96 = (f32[17,32,128]{2,1,0:T(8,128)}, f32[17,17]{1,0:T(8,128)}) custom-call(f32[17,32,128]{2,1,0:T(8,128)S(1)} %get-tuple-element.4.basis, f32[17,17]{1,0:T(8,128)S(1)} %get-tuple-element.5.gram), custom_call_target="tpu_custom_call" | custom-call | tf_op jit(solution)/shard_map/pallas_call | solution.py:474

commit v6 on v5

--- a/solution.py
+++ b/solution.py
@@ -331,12 +331,13 @@
 
     lax.fori_loop(0, depth // 2, pair, 0)
 
-    last = jnp.zeros((GROWS, bs), jnp.float32)
+    lasts = [jnp.zeros((GROWS, bs), jnp.float32)] * 4
     square = jnp.zeros((1, bs), jnp.float32)
     for b in range(rows):
         new = ext_a[2 * b : 2 * b + 1, :]
-        last = last + fields[b] * new
+        lasts[b % 4] = lasts[b % 4] + fields[b] * new
         square = square + new * new
+    last = (lasts[0] + lasts[1]) + (lasts[2] + lasts[3])
     at = lax.broadcasted_iota(jnp.int32, (GROWS, bs), 0)
     last = jnp.where(at == depth, square, last)
     row_mine[...] = jnp.zeros((1, bs), jnp.float32)

time: 57.6 us -> 57.6 us (level)
  no operation moved by 1% of the time
where the time goes in v6:
time: 57.6 us; the launch traced here: 57.4 us
  Pallas kernels  56.8 us (99%)
  between operations  0.64 us (1%)
    pallas_call x1, Pallas kernels, per_device(): pl.pallas_call(functools.partial(kernel, rows, slots, bs, halo, depth, n_...  56 us

profile of v6, /device:TPU:1, one launch (start us, length us, event | category | flops | bytes accessed | tf_op | source)
XLA Modules:
  0.0 57.4 jit_solution(2519802005561503571)
XLA Ops:
  0.6 56.0 %shard_map.95 = (f32[17,32,128]{2,1,0:T(8,128)S(1)}, f32[17,17]{1,0:T(8,128)S(1)}) custom-call(f32[32,128]{1,0:T(8,128)} %p_hbm.1, f32[32,128]{1,0:T(8,128)} %r_hbm.1, f32[32,128]{1,0:T(8,128)} %diag_hbm.1, f32[8]{0:T(128)} %shifts_hbm.1, f32[32,6,128,128]{3,2,1,0:T(8,128)} %values_hbm.1, s32[6,32]{1,0:T(8,128)} %bitcast.1, s32[32]{0:T(128)} %live_hbm.1, ...), custom_call_target="tpu_custom_call" | custom-call | tf_op jit(solution)/shard_map/pallas_call | solution.py:431
  56.7 0.7 %shard_map.96 = (f32[17,32,128]{2,1,0:T(8,128)}, f32[17,17]{1,0:T(8,128)}) custom-call(f32[17,32,128]{2,1,0:T(8,128)S(1)} %get-tuple-element.4.basis, f32[17,17]{1,0:T(8,128)S(1)} %get-tuple-element.5.gram), custom_call_target="tpu_custom_call" | custom-call | tf_op jit(solution)/shard_map/pallas_call | solution.py:475
